TPU v7x, 32 devices: a whole 2x2x4 slice. The times are simulated.
32 devices in a mesh: group: 4 (over y, x), shard: 8 (over z, core).
Axes of the slice: x: 2, y: 2, z: 4, core: 2. Of those that a mesh axis runs over, the one named last changes fastest.
Arguments:
- amplitudes: float32 [32768, 128], P(('group', 'shard')), may hold values from -6 to 6
- orbit_index: int32 [32768, 128], P(('group', 'shard')), may hold values from 0 to 5
- requests: int32 [32, 32, 2], P(('group', 'shard')), may hold values from 0 to 1024, as said below
- targets: int32 [32, 32, 2], P(('group', 'shard')), may hold values from 0 to 1023
Outputs:
- image: float32 [32768, 128], P(('group', 'shard'))
Inputs may be any that keep to these rules, and one draw needn't show every extreme that they name: `requests`: each value is an owner's local block number below 1024, or 1024 for an empty slot; in every list from one requester to one owner the used slots come first; every draw has owners whose lists from every requester are full (2 blocks).
All inputs are finite; a program needn't handle non-finite values.
Results may differ from a plain program's by a relative error of at most 0.0003.
Values sent between devices are 32-bit elements; how exact they have to be, the bound alone decides.
A program may use at most 64 MiB of HBM per device.

v0:
```python
import jax
import jax.numpy as jnp
from jax import lax
from jax.sharding import PartitionSpec as P


def per_device(amplitudes, orbit_index, requests, targets):
    blocks = amplitudes.shape[0]
    columns = amplitudes.shape[1]
    groups = lax.axis_size("group")
    shards = lax.axis_size("shard")
    factor = jnp.sqrt(96.0 * jnp.exp2(-orbit_index.astype(jnp.float32)))
    weighted = amplitudes * factor
    padded = jnp.concatenate([weighted, jnp.zeros((1, columns), jnp.float32)], axis=0)
    wanted = requests.reshape(groups, shards, -1)
    places = targets.reshape(groups, shards, -1)
    own_rows = weighted[places]
    incoming = lax.all_to_all(
        lax.all_to_all(wanted, "group", split_axis=0, concat_axis=0, tiled=True),
        "shard",
        split_axis=1,
        concat_axis=1,
        tiled=True,
    )
    received = lax.all_to_all(
        lax.all_to_all(own_rows, "group", split_axis=0, concat_axis=0, tiled=True),
        "shard",
        split_axis=1,
        concat_axis=1,
        tiled=True,
    )
    served = padded[incoming]
    arrived = lax.all_to_all(
        lax.all_to_all(served, "group", split_axis=0, concat_axis=0, tiled=True),
        "shard",
        split_axis=1,
        concat_axis=1,
        tiled=True,
    )
    pulled = jax.ops.segment_sum(
        arrived.reshape(-1, columns), places.reshape(-1), num_segments=blocks
    )
    pushed = jax.ops.segment_sum(
        received.reshape(-1, columns), incoming.reshape(-1), num_segments=blocks + 1
    )
    return (pulled + pushed[:blocks]) / factor


def solution(mesh):
    return jax.shard_map(
        per_device,
        mesh=mesh,
        in_specs=(
            P(("group", "shard"), None),
            P(("group", "shard"), None),
            P(("group", "shard"), None, None),
            P(("group", "shard"), None, None),
        ),
        out_specs=P(("group", "shard"), None),
        check_vma=False,
    )
```

profile of v0, /device:TPU:0, one launch (start us, length us, event | category | flops | bytes accessed | tf_op | source)
XLA Modules:
  0.0 58.8 jit_solution(16126421621378465620)
XLA Ops:
  0.0 0.8 %reshape.40 = s32[4,8,2]{1,0,2:T(4,128)S(1)} reshape(s32[1,32,2]{1,2,0:T(2,128)} %param.6) | data formatting | bytes 512 | tf_op jit(solution)/shard_map/reshape | solution.py:15
  0.8 0.6 %copy.23 = s32[4,8,2]{1,2,0:T(2,128)} copy(s32[4,8,2]{1,0,2:T(4,128)S(1)} %reshape.40) | data formatting | bytes 512 | tf_op jit(solution)/shard_map/reshape | solution.py:15
  1.4 0.0 copy-start.1
  1.4 5.3 %all-to-all-start = ((s32[4,8,2]{1,2,0:T(2,128)}), s32[4,8,2]{1,2,0:T(2,128)S(1)}, u32[]{:S(2)}, u32[]{:S(2)}) async-start(s32[4,8,2]{1,2,0:T(2,128)} %copy.23), calls=%async_computation | async-start | bytes 8192 | tf_op jit(solution)/shard_map/all_to_all | solution.py:19
  6.7 0.0 copy-done.1
  6.7 0.1 reshape.41
  6.8 1.4 %fusion.1 = f32[1024,128]{1,0:T(8,128)S(1)} fusion(f32[1024,128]{1,0:T(8,128)} %param.4, s32[1024,128]{1,0:T(8,128)} %param.5), kind=kLoop, calls=%fused_computation.6 | loop fusion | flops 655360 | bytes 1572864 | tf_op jit(solution)/shard_map/mul | solution.py:13
  8.2 0.1 copy.26
  8.3 0.1 reshape.46
  8.4 2.9 %all-to-all-done = s32[4,8,2]{1,2,0:T(2,128)S(1)} async-done(((s32[4,8,2]{1,2,0:T(2,128)}), s32[4,8,2]{1,2,0:T(2,128)S(1)}, u32[]{:S(2)}, u32[]{:S(2)}) %all-to-all-start) | async-done | bytes 288 | tf_op jit(solution)/shard_map/all_to_all | solution.py:19
  11.4 0.7 %copy.24 = s32[4,8,2]{0,2,1:T(2,128)} copy(s32[4,8,2]{1,2,0:T(2,128)S(1)} %all-to-all-done) | data formatting | bytes 512 | tf_op jit(solution)/shard_map/all_to_all | solution.py:19
  12.0 4.9 %all-to-all-start.1 = ((s32[4,8,2]{0,2,1:T(2,128)}), s32[4,8,2]{0,2,1:T(2,128)S(1)}, u32[]{:S(2)}, u32[]{:S(2)}) async-start(s32[4,8,2]{0,2,1:T(2,128)} %copy.24), calls=%async_computation.1 | async-start | bytes 16384 | tf_op jit(solution)/shard_map/all_to_all | solution.py:18
  16.9 1.2 %gather_fusion = f32[64,128]{1,0:T(8,128)} fusion(f32[1024,128]{1,0:T(8,128)S(1)} %fusion.1, s32[1024]{0:T(1024)S(1)} %pad_clamp_fusion.1), kind=kCustom, calls=%fused_computation | custom fusion | bytes 65792 | tf_op jit(solution)/shard_map/gather | solution.py:17
  18.2 4.4 %all-to-all-done.1 = s32[4,8,2]{0,2,1:T(2,128)S(1)} async-done(((s32[4,8,2]{0,2,1:T(2,128)}), s32[4,8,2]{0,2,1:T(2,128)S(1)}, u32[]{:S(2)}, u32[]{:S(2)}) %all-to-all-start.1) | async-done | bytes 288 | tf_op jit(solution)/shard_map/all_to_all | solution.py:18
  22.5 3.3 %all-to-all-start.2 = ((f32[4,8,2,128]{3,2,1,0:T(2,128)}), f32[4,8,2,128]{3,2,1,0:T(2,128)S(1)}, u32[]{:S(2)}, u32[]{:S(2)}) async-start(f32[4,8,2,128]{3,2,1,0:T(2,128)} %bitcast), calls=%async_computation.2 | async-start | bytes 65536 | tf_op jit(solution)/shard_map/all_to_all | solution.py:26
  25.8 0.1 copy.30
  26.0 0.1 reshape.54
  26.1 1.2 %gather_fusion.1 = f32[64,128]{1,0:T(8,128)} fusion(f32[1025,128]{1,0:T(8,128)S(1)} %concatenate.3, s32[1024]{0:T(1024)S(1)} %pad_clamp_fusion), kind=kCustom, calls=%fused_computation.1 | custom fusion | bytes 65792 | tf_op jit(solution)/shard_map/gather | solution.py:32
  27.3 3.3 %all-to-all-done.2 = f32[4,8,2,128]{3,2,1,0:T(2,128)S(1)} async-done(((f32[4,8,2,128]{3,2,1,0:T(2,128)}), f32[4,8,2,128]{3,2,1,0:T(2,128)S(1)}, u32[]{:S(2)}, u32[]{:S(2)}) %all-to-all-start.2) | async-done | bytes 32800 | tf_op jit(solution)/shard_map/all_to_all | solution.py:26
  30.5 3.3 %all-to-all-start.4 = ((f32[4,8,2,128]{3,2,1,0:T(2,128)}), f32[4,8,2,128]{3,2,1,0:T(2,128)S(1)}, u32[]{:S(2)}, u32[]{:S(2)}) async-start(f32[4,8,2,128]{3,2,1,0:T(2,128)} %bitcast.2), calls=%async_computation.4 | async-start | bytes 65536 | tf_op jit(solution)/shard_map/all_to_all | solution.py:34
  33.8 0.6 %copy.27 = f32[4,8,2,128]{3,2,0,1:T(2,128)} copy(f32[4,8,2,128]{3,2,1,0:T(2,128)S(1)} %all-to-all-done.2) | data formatting | bytes 65536 | tf_op jit(solution)/shard_map/all_to_all | solution.py:26
  34.4 4.1 %all-to-all-done.4 = f32[4,8,2,128]{3,2,1,0:T(2,128)S(1)} async-done(((f32[4,8,2,128]{3,2,1,0:T(2,128)}), f32[4,8,2,128]{3,2,1,0:T(2,128)S(1)}, u32[]{:S(2)}, u32[]{:S(2)}) %all-to-all-start.4) | async-done | bytes 32800 | tf_op jit(solution)/shard_map/all_to_all | solution.py:34
  38.5 3.3 %all-to-all-start.3 = ((f32[4,8,2,128]{3,2,0,1:T(2,128)}), f32[4,8,2,128]{3,2,0,1:T(2,128)S(1)}, u32[]{:S(2)}, u32[]{:S(2)}) async-start(f32[4,8,2,128]{3,2,0,1:T(2,128)} %copy.27), calls=%async_computation.3 | async-start | bytes 65536 | tf_op jit(solution)/shard_map/all_to_all | solution.py:25
  41.9 0.6 %copy.31 = f32[4,8,2,128]{3,2,0,1:T(2,128)} copy(f32[4,8,2,128]{3,2,1,0:T(2,128)S(1)} %all-to-all-done.4) | data formatting | bytes 65536 | tf_op jit(solution)/shard_map/all_to_all | solution.py:34
  42.5 5.1 %all-to-all-done.3 = f32[4,8,2,128]{3,2,0,1:T(2,128)S(1)} async-done(((f32[4,8,2,128]{3,2,0,1:T(2,128)}), f32[4,8,2,128]{3,2,0,1:T(2,128)S(1)}, u32[]{:S(2)}, u32[]{:S(2)}) %all-to-all-start.3) | async-done | bytes 32800 | tf_op jit(solution)/shard_map/all_to_all | solution.py:25
  47.5 3.3 %all-to-all-start.5 = ((f32[4,8,2,128]{3,2,0,1:T(2,128)}), f32[4,8,2,128]{3,2,0,1:T(2,128)S(1)}, u32[]{:S(2)}, u32[]{:S(2)}) async-start(f32[4,8,2,128]{3,2,0,1:T(2,128)} %copy.31), calls=%async_computation.5 | async-start | bytes 65536 | tf_op jit(solution)/shard_map/all_to_all | solution.py:33
  50.9 0.1 copy.29
  51.0 0.1 reshape.70
  51.1 0.1 copy.25
  51.2 0.1 reshape.62
  51.4 0.9 %scatter_custom_fusion = f32[1025,128]{1,0:T(8,128)S(1)} fusion(s32[64]{0:T(128)S(1)} %reshape.62, f32[64,128]{1,0:T(8,128)S(1)} %bitcast.13, f32[]{:T(128)} %constant.6.clone.1), kind=kCustom, calls=%fused_computation.7 | custom fusion | flops 8192 | bytes 524804 | tf_op jit(solution)/shard_map/scatter-add | solution.py:43
  52.3 0.0 copy-start
  52.3 4.2 %all-to-all-done.5 = f32[4,8,2,128]{3,2,0,1:T(2,128)S(1)} async-done(((f32[4,8,2,128]{3,2,0,1:T(2,128)}), f32[4,8,2,128]{3,2,0,1:T(2,128)S(1)}, u32[]{:S(2)}, u32[]{:S(2)}) %all-to-all-start.5) | async-done | bytes 32800 | tf_op jit(solution)/shard_map/all_to_all | solution.py:33
  56.6 1.1 %scatter_fusion = f32[1024,128]{1,0:T(8,128)S(1)} fusion(f32[1024,128]{1,0:T(8,128)S(1)} %slice.8, s32[64]{0:T(128)S(1)} %reshape.70, f32[64,128]{1,0:T(8,128)S(1)} %bitcast.12), kind=kCustom, calls=%fused_computation.3 | custom fusion | flops 8192 | bytes 98560 | tf_op jit(solution)/shard_map/scatter-add | solution.py:40
  57.7 0.0 copy-done
  57.7 1.0 %fusion = f32[1024,128]{1,0:T(8,128)} fusion(f32[1024,128]{1,0:T(8,128)S(1)} %scatter_fusion, s32[1024,128]{1,0:T(8,128)S(1)} %copy-done), kind=kLoop, calls=%fused_computation.5 | loop fusion | flops 655360 | bytes 1572864 | tf_op jit(solution)/shard_map/div | solution.py:46
  (8 shorter events, 0.1 us)
Async XLA Ops:
  1.4 5.3 %copy-start.1 = (s32[1,32,2]{1,2,0:T(2,128)S(1)}, s32[1,32,2]{1,2,0:T(2,128)}, u32[]{:S(2)}) copy-start(s32[1,32,2]{1,2,0:T(2,128)} %param.7) | copy-start | bytes 772
  1.4 10.0 %all-to-all-start = ((s32[4,8,2]{1,2,0:T(2,128)}), s32[4,8,2]{1,2,0:T(2,128)S(1)}, u32[]{:S(2)}, u32[]{:S(2)}) async-start(s32[4,8,2]{1,2,0:T(2,128)} %copy.23), calls=%async_computation | async-start | bytes 8192 | tf_op jit(solution)/shard_map/all_to_all | solution.py:19
  12.0 10.5 %all-to-all-start.1 = ((s32[4,8,2]{0,2,1:T(2,128)}), s32[4,8,2]{0,2,1:T(2,128)S(1)}, u32[]{:S(2)}, u32[]{:S(2)}) async-start(s32[4,8,2]{0,2,1:T(2,128)} %copy.24), calls=%async_computation.1 | async-start | bytes 16384 | tf_op jit(solution)/shard_map/all_to_all | solution.py:18
  22.5 8.0 %all-to-all-start.2 = ((f32[4,8,2,128]{3,2,1,0:T(2,128)}), f32[4,8,2,128]{3,2,1,0:T(2,128)S(1)}, u32[]{:S(2)}, u32[]{:S(2)}) async-start(f32[4,8,2,128]{3,2,1,0:T(2,128)} %bitcast), calls=%async_computation.2 | async-start | bytes 65536 | tf_op jit(solution)/shard_map/all_to_all | solution.py:26
  30.5 8.0 %all-to-all-start.4 = ((f32[4,8,2,128]{3,2,1,0:T(2,128)}), f32[4,8,2,128]{3,2,1,0:T(2,128)S(1)}, u32[]{:S(2)}, u32[]{:S(2)}) async-start(f32[4,8,2,128]{3,2,1,0:T(2,128)} %bitcast.2), calls=%async_computation.4 | async-start | bytes 65536 | tf_op jit(solution)/shard_map/all_to_all | solution.py:34
  38.5 9.0 %all-to-all-start.3 = ((f32[4,8,2,128]{3,2,0,1:T(2,128)}), f32[4,8,2,128]{3,2,0,1:T(2,128)S(1)}, u32[]{:S(2)}, u32[]{:S(2)}) async-start(f32[4,8,2,128]{3,2,0,1:T(2,128)} %copy.27), calls=%async_computation.3 | async-start | bytes 65536 | tf_op jit(solution)/shard_map/all_to_all | solution.py:25
  47.5 9.0 %all-to-all-start.5 = ((f32[4,8,2,128]{3,2,0,1:T(2,128)}), f32[4,8,2,128]{3,2,0,1:T(2,128)S(1)}, u32[]{:S(2)}, u32[]{:S(2)}) async-start(f32[4,8,2,128]{3,2,0,1:T(2,128)} %copy.31), calls=%async_computation.5 | async-start | bytes 65536 | tf_op jit(solution)/shard_map/all_to_all | solution.py:33
  52.3 5.4 %copy-start = (s32[1024,128]{1,0:T(8,128)S(1)}, s32[1024,128]{1,0:T(8,128)}, u32[]{:S(2)}) copy-start(s32[1024,128]{1,0:T(8,128)} %param.5) | copy-start | bytes 1572868
where the time goes:
time: 59.3 us; the launch traced here: 58.8 us
  waiting for transfers between devices  24 us (40%)
  starting transfers between devices  23.4 us (39%)
  local copies, waits for them, and re-layouts  6.72 us (11%)
  other arithmetic  4.53 us (8%)
    all_to_all x1, starting transfers between devices, per_device(): lax.all_to_all(wanted, 'group', split_axis=0, concat_axis=0, tiled=True)  5.32 us
    all_to_all x1, waiting for transfers between devices, per_device(): lax.all_to_all(lax.all_to_all(own_rows, 'group', split_axis=0, concat_axi...  5.05 us
    all_to_all x1, starting transfers between devices, per_device(): lax.all_to_all(lax.all_to_all(wanted, 'group', split_axis=0, concat_axis=...  4.88 us
    all_to_all x1, waiting for transfers between devices, per_device(): lax.all_to_all(lax.all_to_all(wanted, 'group', split_axis=0, concat_axis=...  4.37 us
    all_to_all x1, waiting for transfers between devices, per_device(): lax.all_to_all(lax.all_to_all(served, 'group', split_axis=0, concat_axis=...  4.24 us
    all_to_all x1, waiting for transfers between devices, per_device(): lax.all_to_all(served, 'group', split_axis=0, concat_axis=0, tiled=True)  4.1 us
    all_to_all x1, starting transfers between devices, per_device(): lax.all_to_all(lax.all_to_all(own_rows, 'group', split_axis=0, concat_axi...  3.34 us
    all_to_all x1, starting transfers between devices, per_device(): lax.all_to_all(lax.all_to_all(served, 'group', split_axis=0, concat_axis=...  3.34 us
  transfers between devices with their start and end apart: 6, of which 6 were waited for; matrix products, arithmetic and copies ran while one was open for 12% of the time, Pallas kernels for 0%

commit v1 on v0

v1 whole, which is shorter than its diff:
```python
import functools

import jax
import jax.numpy as jnp
from jax import lax
from jax.experimental import pallas as pl
from jax.experimental.pallas import tpu as pltpu
from jax.sharding import PartitionSpec as P

MESH = pl.DeviceIdType.MESH


def split(x):
    hi = x.astype(jnp.bfloat16)
    lo = (x - hi.astype(jnp.float32)).astype(jnp.bfloat16)
    return jnp.concatenate([hi, lo], axis=1)


def kernel(groups, shards, cap, req_hbm, tgt_hbm, amp_hbm, orb_hbm, out_ref,
           req, tgt, amp, orb, inv, halves, onehot, ids_out, rows_out, back_out, ids_in, rows_in,
           load_sem, ids_send, ids_recv, rows_send, rows_recv, back_send, back_recv):
    ranks = groups * shards
    slots = ranks * cap
    blocks, lanes = amp.shape
    me_g, me_s = lax.axis_index("group"), lax.axis_index("shard")
    me = me_g * shards + me_s

    loads = [
        pltpu.make_async_copy(src, dst, load_sem.at[i])
        for i, (src, dst) in enumerate(((req_hbm, req), (tgt_hbm, tgt), (amp_hbm, amp), (orb_hbm, orb)))
    ]
    for load in loads:
        load.start()

    def peer(k):
        rank = lax.rem(me + k, ranks)
        return rank, (lax.div(rank, shards), lax.rem(rank, shards))

    barrier = pltpu.get_barrier_semaphore()

    def greet(k, carry):
        pl.semaphore_signal(barrier, inc=1, device_id=peer(k)[1], device_id_type=MESH)
        return carry

    lax.fori_loop(1, ranks, greet, 0)

    loads[0].wait()
    loads[1].wait()

    def spread(o, carry):
        for c in range(cap):
            ids_out[o, c:c + 1, :] = jnp.full((1, lanes), req[0, c, o], jnp.int32)
            ids_in[ranks + o, c:c + 1, :] = jnp.full((1, lanes), tgt[0, c, o], jnp.int32)
        return carry

    lax.fori_loop(0, ranks, spread, 0, unroll=4)
    ids_in[me] = ids_out[me]
    pl.semaphore_wait(barrier, ranks - 1)

    def exchange(src, dst, base, send_sem, recv_sem):
        def body(k, carry):
            rank, device = peer(k)
            pltpu.make_async_remote_copy(
                src_ref=src.at[rank], dst_ref=dst.at[base + me], send_sem=send_sem, recv_sem=recv_sem,
                device_id=device, device_id_type=MESH,
            ).start()
            return carry

        lax.fori_loop(1, ranks, body, 0)

    def wait_all(ref, sem):
        part = ref.at[pl.ds(0, ranks - 1)]
        pltpu.make_async_copy(part, part, sem).wait()

    exchange(ids_out, ids_in, 0, ids_send, ids_recv)
    loads[2].wait()
    loads[3].wait()
    level = orb[...].astype(jnp.float32)
    factor = jnp.sqrt(96.0 * jnp.exp2(-level))
    halves[...] = split(amp[...] * factor)
    inv[...] = 1.0 / factor

    def gather(ids):
        place = lax.broadcasted_iota(jnp.int32, (slots, blocks), 1)
        wanted = jnp.concatenate([ids] * (blocks // lanes), axis=1)
        picks = jnp.where(place == wanted, 1.0, 0.0).astype(jnp.bfloat16)
        both = jnp.dot(picks, halves[...], preferred_element_type=jnp.float32)
        return (both[:, :lanes] + both[:, lanes:]).reshape(ranks, cap, lanes)

    rows_out[...] = gather(ids_in[ranks:].reshape(slots, lanes))
    rows_in[me] = rows_out[me]
    exchange(rows_out, rows_in, 0, rows_send, rows_recv)

    wait_all(ids_in, ids_recv)
    back_out[...] = gather(ids_in[:ranks].reshape(slots, lanes))
    rows_in[ranks + me] = back_out[me]
    exchange(back_out, rows_in, ranks, back_send, back_recv)

    ids = ids_in[...].reshape(2 * slots, lanes)
    for start in range(0, 2 * slots, lanes):
        part = ids[start:start + lanes]
        diagonal = lax.broadcasted_iota(jnp.int32, (lanes, lanes), 0) == lax.broadcasted_iota(
            jnp.int32, (lanes, lanes), 1
        )
        line = jnp.sum(jnp.where(diagonal, part, 0), axis=0, keepdims=True)
        place = lax.broadcasted_iota(jnp.int32, (blocks, lanes), 0)
        onehot[:, start:start + lanes] = jnp.where(place == line, 1.0, 0.0).astype(jnp.bfloat16)

    wait_all(rows_in, rows_recv)
    wait_all(rows_in, back_recv)
    rows = split(rows_in[...].reshape(2 * slots, lanes))
    both = jnp.dot(onehot[...], rows, preferred_element_type=jnp.float32)
    out_ref[...] = (both[:, :lanes] + both[:, lanes:]) * inv[...]
    wait_all(ids_out, ids_send)
    wait_all(rows_out, rows_send)
    wait_all(back_out, back_send)


def per_device(amplitudes, orbit_index, requests, targets):
    groups = lax.axis_size("group")
    shards = lax.axis_size("shard")
    ranks = groups * shards
    cap = requests.shape[-1]
    blocks, lanes = amplitudes.shape
    slot_rows = (ranks, cap, lanes)
    both_rows = (2 * ranks, cap, lanes)
    anywhere = pl.BlockSpec(memory_space=pl.ANY)
    return pl.pallas_call(
        functools.partial(kernel, groups, shards, cap),
        out_shape=jax.ShapeDtypeStruct((blocks, lanes), jnp.float32),
        in_specs=[anywhere] * 4,
        out_specs=pl.BlockSpec(memory_space=pltpu.VMEM),
        scratch_shapes=[
            pltpu.SMEM((1, cap, ranks), jnp.int32),
            pltpu.SMEM((1, cap, ranks), jnp.int32),
            pltpu.VMEM((blocks, lanes), jnp.float32),
            pltpu.VMEM((blocks, lanes), jnp.int32),
            pltpu.VMEM((blocks, lanes), jnp.float32),
            pltpu.VMEM((blocks, 2 * lanes), jnp.bfloat16),
            pltpu.VMEM((blocks, 2 * ranks * cap), jnp.bfloat16),
            pltpu.VMEM(slot_rows, jnp.int32),
            pltpu.VMEM(slot_rows, jnp.float32),
            pltpu.VMEM(slot_rows, jnp.float32),
            pltpu.VMEM(both_rows, jnp.int32),
            pltpu.VMEM(both_rows, jnp.float32),
            pltpu.SemaphoreType.DMA((4,)),
        ] + [pltpu.SemaphoreType.DMA] * 6,
        compiler_params=pltpu.CompilerParams(collective_id=0, has_side_effects=True),
        name="couple",
    )(requests.transpose(0, 2, 1), targets.transpose(0, 2, 1), amplitudes, orbit_index)


def solution(mesh):
    return jax.shard_map(
        per_device,
        mesh=mesh,
        in_specs=(
            P(("group", "shard"), None),
            P(("group", "shard"), None),
            P(("group", "shard"), None, None),
            P(("group", "shard"), None, None),
        ),
        out_specs=P(("group", "shard"), None),
        check_vma=False,
    )
```

time: 59.3 us -> 19.7 us (0.33)
  waiting for transfers between devices: 24 us -> 0 us
  starting transfers between devices: 23.4 us -> 0 us
  Pallas kernels: 0 us -> 17.6 us
  local copies, waits for them, and re-layouts: 6.72 us -> 1.87 us
  other arithmetic: 4.53 us -> 0 us
    all_to_all x6 -> x0, waiting for transfers between devices: 24 us -> none  [the longest x1 5.05 us: per_device(): lax.all_to_all(lax.all_to_all(own_rows, 'group', split_axis=0, concat_axi...]
    all_to_all x6 -> x0, starting transfers between devices: 23.4 us -> none  [the longest x1 5.32 us: per_device(): lax.all_to_all(wanted, 'group', split_axis=0, concat_axis=0, tiled=True)]
    pallas_call x0 -> x1, Pallas kernels: none -> 17.6 us  [per_device(): pl.pallas_call(functools.partial(kernel, groups, shards, cap), out_shape=...]
    gather x2 -> x0, local copies, waits for them, and re-layouts: 2.38 us -> none  [the longest x1 1.19 us: per_device(): own_rows = weighted[places]]
    all_to_all x6 -> x0, local copies, waits for them, and re-layouts: 2.08 us -> none  [the longest x1 0.68 us: per_device(): lax.all_to_all(wanted, 'group', split_axis=0, concat_axis=0, tiled=True)]
    scatter-add x2 -> x0, other arithmetic: 2.03 us -> none  [the longest x1 1.12 us: per_device(): jax.ops.segment_sum(arrived.reshape(-1, columns), places.reshape(-1), num...]
    unnamed x5 -> x1, local copies, waits for them, and re-layouts: 0.1 us -> 1.87 us
    reshape x3 -> x0, local copies, waits for them, and re-layouts: 1.44 us -> none  [the longest x2 1.36 us: per_device(): wanted = requests.reshape(groups, shards, -1)]
  transfers between devices with their start and end apart: 6 -> 0, of which waited for: 6 -> 0; matrix products, arithmetic and copies ran while one was open for 12% -> 0% of each run, Pallas kernels for 0% -> 0%
where the time goes in v1:
time: 19.7 us; the launch traced here: 19.5 us
  Pallas kernels  17.6 us (89%)
  local copies, waits for them, and re-layouts  1.87 us (9%)
    pallas_call x1, Pallas kernels, per_device(): pl.pallas_call(functools.partial(kernel, groups, shards, cap), out_shape=...  17.6 us
    unnamed x1, local copies, waits for them, and re-layouts  1.87 us

profile of v1, /device:TPU:0, one launch (start us, length us, event | category | flops | bytes accessed | tf_op | source)
XLA Modules:
  0.0 19.5 jit_solution(4340202890544795641)
XLA Ops:
  0.0 17.6 %couple.1 = f32[1024,128]{1,0:T(8,128)} custom-call(s32[1,2,32]{2,1,0:T(2,128)} %bitcast.2, s32[1,2,32]{2,1,0:T(2,128)} %bitcast.3, f32[1024,128]{1,0:T(8,128)} %amp_hbm.1, s32[1024,128]{1,0:T(8,128)} %orb_hbm.1), custom_call_target="tpu_custom_call" | custom-call | tf_op jit(solution)/shard_map/couple/pallas_call | solution.py:128
  17.6 1.9 %copy.6 = f32[1024,128]{1,0:T(8,128)} copy(f32[1024,128]{1,0:T(8,128)} %couple.1) | data formatting | bytes 1048576

commit v2 on v1

--- a/solution.py
+++ b/solution.py
@@ -25,16 +25,13 @@
     me_g, me_s = lax.axis_index("group"), lax.axis_index("shard")
     me = me_g * shards + me_s
 
-    loads = [
-        pltpu.make_async_copy(src, dst, load_sem.at[i])
-        for i, (src, dst) in enumerate(((req_hbm, req), (tgt_hbm, tgt), (amp_hbm, amp), (orb_hbm, orb)))
-    ]
-    for load in loads:
-        load.start()
+    upper = (me >= ranks // 2).astype(jnp.int32)
+    mirror = upper * me + (1 - upper) * (ranks - 1 - me)
 
     def peer(k):
-        rank = lax.rem(me + k, ranks)
-        return rank, (lax.div(rank, shards), lax.rem(rank, shards))
+        skipped = k + (k >= mirror).astype(jnp.int32)
+        rank = upper * skipped + (1 - upper) * (ranks - 1 - skipped)
+        return rank, (rank // shards, rank % shards)
 
     barrier = pltpu.get_barrier_semaphore()
 
@@ -42,7 +39,14 @@
         pl.semaphore_signal(barrier, inc=1, device_id=peer(k)[1], device_id_type=MESH)
         return carry
 
-    lax.fori_loop(1, ranks, greet, 0)
+    lax.fori_loop(0, ranks - 1, greet, 0)
+
+    loads = [
+        pltpu.make_async_copy(src, dst, load_sem.at[i])
+        for i, (src, dst) in enumerate(((req_hbm, req), (tgt_hbm, tgt), (amp_hbm, amp), (orb_hbm, orb)))
+    ]
+    for load in loads:
+        load.start()
 
     loads[0].wait()
     loads[1].wait()
@@ -66,7 +70,7 @@
             ).start()
             return carry
 
-        lax.fori_loop(1, ranks, body, 0)
+        lax.fori_loop(0, ranks - 1, body, 0)
 
     def wait_all(ref, sem):
         part = ref.at[pl.ds(0, ranks - 1)]
@@ -124,7 +128,7 @@
     blocks, lanes = amplitudes.shape
     slot_rows = (ranks, cap, lanes)
     both_rows = (2 * ranks, cap, lanes)
-    anywhere = pl.BlockSpec(memory_space=pl.ANY)
+    anywhere = pl.BlockSpec(memory_space=pltpu.HBM)
     return pl.pallas_call(
         functools.partial(kernel, groups, shards, cap),
         out_shape=jax.ShapeDtypeStruct((blocks, lanes), jnp.float32),
@@ -145,9 +149,9 @@
             pltpu.VMEM(both_rows, jnp.float32),
             pltpu.SemaphoreType.DMA((4,)),
         ] + [pltpu.SemaphoreType.DMA] * 6,
-        compiler_params=pltpu.CompilerParams(collective_id=0, has_side_effects=True),
+        compiler_params=pltpu.CompilerParams(collective_id=0, has_side_effects=True, vmem_limit_bytes=32*1024*1024),
         name="couple",
-    )(requests.transpose(0, 2, 1), targets.transpose(0, 2, 1), amplitudes, orbit_index)
+    )(*(pltpu.with_memory_space_constraint(x, pltpu.HBM) for x in (requests.transpose(0, 2, 1), targets.transpose(0, 2, 1), amplitudes, orbit_index)))
 
 
 def solution(mesh):

time: 19.7 us -> 17.3 us (0.88)
  Pallas kernels: 17.6 us -> 16.4 us
  local copies, waits for them, and re-layouts: 1.87 us -> 0.8 us
    pallas_call x1, Pallas kernels: 17.6 us -> 16.4 us  [per_device(): pl.pallas_call(functools.partial(kernel, groups, shards, cap), out_shape=...]
    unnamed x1, local copies, waits for them, and re-layouts: 1.87 us -> 0.8 us
where the time goes in v2:
time: 17.3 us; the launch traced here: 17.2 us
  Pallas kernels  16.4 us (95%)
  local copies, waits for them, and re-layouts  0.8 us (5%)
    pallas_call x1, Pallas kernels, per_device(): pl.pallas_call(functools.partial(kernel, groups, shards, cap), out_shape=...  16.4 us
    unnamed x1, local copies, waits for them, and re-layouts  0.8 us

profile of v2, /device:TPU:0, one launch (start us, length us, event | category | flops | bytes accessed | tf_op | source)
XLA Modules:
  0.0 17.2 jit_solution(14040456304649998611)
XLA Ops:
  0.0 16.4 %couple.1 = f32[1024,128]{1,0:T(8,128)S(1)} custom-call(s32[1,2,32]{2,1,0:T(2,128)} %bitcast.2, s32[1,2,32]{2,1,0:T(2,128)} %bitcast.3, f32[1024,128]{1,0:T(8,128)} %amp_hbm.1, s32[1024,128]{1,0:T(8,128)} %orb_hbm.1), custom_call_target="tpu_custom_call" | custom-call | tf_op jit(solution)/shard_map/couple/pallas_call | solution.py:132
  16.4 0.8 %copy.6 = f32[1024,128]{1,0:T(8,128)} copy(f32[1024,128]{1,0:T(8,128)S(1)} %couple.1) | data formatting | bytes 1048576

commit v3 on v2

--- a/solution.py
+++ b/solution.py
@@ -39,7 +39,7 @@
         pl.semaphore_signal(barrier, inc=1, device_id=peer(k)[1], device_id_type=MESH)
         return carry
 
-    lax.fori_loop(0, ranks - 1, greet, 0)
+    lax.fori_loop(0, ranks - 1, greet, 0, unroll=4)
 
     loads = [
         pltpu.make_async_copy(src, dst, load_sem.at[i])
@@ -70,7 +70,7 @@
             ).start()
             return carry
 
-        lax.fori_loop(0, ranks - 1, body, 0)
+        lax.fori_loop(0, ranks - 1, body, 0, unroll=4)
 
     def wait_all(ref, sem):
         part = ref.at[pl.ds(0, ranks - 1)]

time: 17.3 us -> 17.4 us (level)
  no operation moved by 1% of the time
where the time goes in v3:
time: 17.4 us; the launch traced here: 17.2 us
  Pallas kernels  16.4 us (94%)
  local copies, waits for them, and re-layouts  0.8 us (5%)
    pallas_call x1, Pallas kernels, per_device(): pl.pallas_call(functools.partial(kernel, groups, shards, cap), out_shape=...  16.4 us
    unnamed x1, local copies, waits for them, and re-layouts  0.8 us

profile of v3, /device:TPU:0, one launch (start us, length us, event | category | flops | bytes accessed | tf_op | source)
XLA Modules:
  0.0 17.2 jit_solution(13798103267120265057)
XLA Ops:
  0.0 16.4 %couple.1 = f32[1024,128]{1,0:T(8,128)S(1)} custom-call(s32[1,2,32]{2,1,0:T(2,128)} %bitcast.2, s32[1,2,32]{2,1,0:T(2,128)} %bitcast.3, f32[1024,128]{1,0:T(8,128)} %amp_hbm.1, s32[1024,128]{1,0:T(8,128)} %orb_hbm.1), custom_call_target="tpu_custom_call" | custom-call | tf_op jit(solution)/shard_map/couple/pallas_call | solution.py:132
  16.4 0.8 %copy.6 = f32[1024,128]{1,0:T(8,128)} copy(f32[1024,128]{1,0:T(8,128)S(1)} %couple.1) | data formatting | bytes 1048576
